TPU v7x, 32 devices: a whole 2x2x4 slice. The times are simulated.
32 devices in a mesh: rows: 32 (over z, y, x, core).
Axes of the slice: x: 2, y: 2, z: 4, core: 2. Of those that a mesh axis runs over, the one named last changes fastest.
Arguments:
- design: bfloat16 [131072, 1024], P('rows'), may hold values from -6 to 6
- weights: float32 [1024], replicated, may hold values from -0.1875 to 0.1875
- labels: int32 [131072], P('rows'), may hold values from 0 to 1
- signs: int32 [131072], P('rows'), may hold values from 0 to 1
- sample_rows: int32 [2048], replicated, may hold values from 0 to 131071
Outputs:
- gradient: float32 [1024], replicated
- newton_step: float32 [1024], replicated
- losses: float32 [4], replicated
All inputs are finite; a program needn't handle non-finite values.
Results may differ from a plain program's by a relative error of at most 0.00085.
The roundings to bfloat16 on the way count: a program that leaves them out, or rounds other values in their place, can miss the bound.
Values may be sent and summed in bfloat16 or wider, within the bound.
A program may use at most 128 MiB of HBM per device.

v0:
```python
import jax
import jax.numpy as jnp
from jax import lax
from jax.sharding import PartitionSpec as P

ridge = 0.05


def hadamard(order_size):
    bits = order_size.bit_length() - 1
    row_index = lax.broadcasted_iota(jnp.int32, (order_size, order_size), 0)
    col_index = lax.broadcasted_iota(jnp.int32, (order_size, order_size), 1)
    parity = jnp.zeros((order_size, order_size), jnp.int32)
    for bit_number in range(bits):
        parity = parity + (row_index >> bit_number & 1) * (col_index >> bit_number & 1)
    return (1 - 2 * (parity % 2)).astype(jnp.float32)


def local_transform(scaled):
    rows_here, width = scaled.shape
    bits = rows_here.bit_length() - 1
    low_order = 1 << bits // 2
    high_order = rows_here // low_order
    high_matrix = hadamard(high_order).astype(jnp.bfloat16)
    first = jnp.dot(
        high_matrix,
        scaled.reshape(high_order, low_order * width),
        preferred_element_type=jnp.float32,
    )
    low_matrix = hadamard(low_order)
    second = jnp.einsum(
        "bx,axd->abd",
        low_matrix,
        first.reshape(high_order, low_order, width),
        precision=lax.Precision.HIGHEST,
    )
    return second.reshape(rows_here, width)


def body(design, weights, labels, signs, sample_rows):
    rows_here, width = design.shape
    device_count = lax.axis_size("rows")
    device_index = lax.axis_index("rows")
    total_rows = rows_here * device_count
    margins = jnp.dot(design, weights.astype(jnp.bfloat16), preferred_element_type=jnp.float32)
    prob = jax.nn.sigmoid(margins)
    target = labels.astype(jnp.float32)
    misfit = (prob - target).astype(jnp.bfloat16)
    grad_part = jnp.dot(misfit, design, preferred_element_type=jnp.float32)
    factor_rows = (1.0 - 2.0 * signs.astype(jnp.float32)) * jnp.sqrt(prob * (1.0 - prob))
    scaled = (design * factor_rows[:, None]).astype(jnp.bfloat16)
    gradient = lax.psum(grad_part, "rows") / total_rows + ridge * weights
    mixed = local_transform(scaled)
    sketch_total = sample_rows.shape[0]
    norm_factor = 1.0 / jnp.sqrt(jnp.float32(sketch_total))
    dev_bits = device_count.bit_length() - 1
    owner = sample_rows // rows_here
    local_rows = sample_rows % rows_here
    parity = jnp.zeros(owner.shape, jnp.int32)
    for bit_number in range(dev_bits):
        parity = parity + (owner >> bit_number & 1) * (device_index >> bit_number & 1)
    coefs = (1 - 2 * (parity % 2)).astype(jnp.float32) * norm_factor
    sketch_own = lax.psum_scatter(
        jnp.take(mixed, local_rows, axis=0) * coefs[:, None],
        "rows",
        scatter_dimension=0,
        tiled=True,
    )
    sketch_low = sketch_own.astype(jnp.bfloat16)
    piece = lax.all_gather(sketch_low, "rows", axis=0, tiled=True)
    gram = jnp.dot(piece.T, piece, preferred_element_type=jnp.float32)
    hessian = gram / total_rows + ridge * jnp.eye(width, dtype=jnp.float32)
    cholesky_factor = jnp.linalg.cholesky(hessian)
    newton_step = jax.scipy.linalg.cho_solve((cholesky_factor, True), gradient)
    along = jnp.dot(design, newton_step.astype(jnp.bfloat16), preferred_element_type=jnp.float32)
    lengths = jnp.array([1.0, 0.5, 0.25, 0.125], jnp.float32)
    trial = margins[None, :] - lengths[:, None] * along[None, :]
    row_loss = jnp.logaddexp(0.0, trial) - target[None, :] * trial
    loss_total = lax.psum(jnp.sum(row_loss, axis=1), "rows")
    moved = weights[None, :] - lengths[:, None] * newton_step[None, :]
    losses = loss_total / total_rows + 0.5 * ridge * jnp.sum(moved * moved, axis=1)
    return (gradient, newton_step, losses)


def solution(mesh):
    placed = (P("rows", None), P(), P("rows"), P("rows"), P())
    return jax.shard_map(
        body, mesh=mesh, in_specs=placed, out_specs=(P(), P(), P()), check_vma=False
    )
```

profile of v0, /device:TPU:0, one launch (start us, length us, event | category | flops | bytes accessed | tf_op | source)
XLA Modules:
  0.0 738.1 jit_solution(15772859127101265802)
XLA Ops:
  23.1 10.6 %reshape.251 = bf16[64,65536]{1,0:T(8,128)(2,1)} reshape(bf16[4096,1024]{1,0:T(8,128)(2,1)} %multiply_convert_fusion) | data formatting | bytes 16777216 | tf_op jit(solution)/shard_map/reshape | solution.py:27
  33.7 11.5 %fusion.2 = f32[64,64,1024]{2,0,1:T(8,128)} fusion(bf16[8,64,8,1024]{3,2,1,0:T(8,128)(2,1)} %bitcast.344, s32[64]{0:T(128)S(1)} %get-tuple-element.83, s32[64]{0:T(128)S(1)} %get-tuple-element.82, s32[64]{0:T(128)S(1)} %get-tuple-element.81, s32[64]{0:T(128)S(1)} %get-tuple-element.80, s32[64]{0:T(128)S(1)} %get-tuple-element.79, s32[64]{0:T(128)S(1)} %get-tuple-element.78), kind=kOutput, calls=%fused_computation.6 | convolution fusion | flops 536977408 | bytes 25167360 | tf_op jit(solution)/shard_map/dot_general | solution.py:25
  45.2 48.2 %fusion = f32[64,1024,64]{1,2,0:T(8,128)} fusion(f32[64,64,1024]{2,0,1:T(8,128)} %fusion.2, s32[64]{0:T(128)S(1)} %get-tuple-element.83, s32[64]{0:T(128)S(1)} %get-tuple-element.82, s32[64]{0:T(128)S(1)} %get-tuple-element.81, s32[64]{0:T(128)S(1)} %get-tuple-element.80, s32[64]{0:T(128)S(1)} %get-tuple-element.79, s32[64]{0:T(128)S(1)} %get-tuple-element.78), kind=kOutput, calls=%fused_computation.3 | convolution fusion | flops 3221327872 | bytes 33555968 | tf_op jit(solution)/shard_map/bx,axd->abd/dot_general | solution.py:31
  93.5 17.5 %gather_fusion = f32[2048,1024]{1,0:T(8,128)} fusion(f32[4096,1024]{1,0:T(8,128)} %bitcast.343, s32[2048]{0:T(1024)S(1)} %broadcast_clamp_fusion), kind=kCustom, calls=%fused_computation | custom fusion | bytes 16785408 | tf_op jit(solution)/shard_map/jit(_take)/gather | solution.py:64
  117.0 152.8 %reduce-scatter.2.cloned.1.call-done = f32[64,1024]{1,0:T(8,128)} async-done(((f32[2048,1024]{1,0:T(8,128)}), f32[64,1024]{1,0:T(8,128)}) %reduce-scatter.2.cloned.1.call-update) | async-done | bytes 262160 | tf_op jit(solution)/shard_map/reduce_scatter | solution.py:63
  276.1 37.1 %psum.14 = f32[1024]{0:T(1024)S(1)} all-reduce(f32[1024]{0:T(1024)S(1)} %bitcast.354), channel_id=1, replica_groups=mesh['rows'=32] {'rows'}, use_global_device_ids=true, to_apply=%region_0.0 | all-reduce | flops 1024 | bytes 8192 | tf_op jit(solution)/shard_map/psum | solution.py:52
  313.1 17.0 %all-gather.2.cloned.1.call-done = bf16[2048,1024]{1,0:T(8,128)(2,1)} async-done(((bf16[64,1024]{1,0:T(8,128)(2,1)}), bf16[2048,1024]{1,0:T(8,128)(2,1)}) %all-gather.2.cloned.1.call-update) | async-done | bytes 4194320 | tf_op jit(solution)/shard_map/all_gather | solution.py:70
  353.8 11.7 %cholesky.222 = f32[128,128]{1,0:T(8,128)S(1)} custom-call(f32[128,128]{1,0:T(8,128)S(1)} %cholesky.577), custom_call_target="Cholesky" | custom-call | tf_op jit(solution)/shard_map/jit(cholesky)/cholesky | solution.py:73
  368.0 9.8 %custom-call.66 = f32[1,128,128]{1,2,0:T(8,128)S(1)} custom-call(f32[1,128,128]{2,1,0:T(8,128)S(1)} %get-tuple-element.42), custom_call_target="InvertDiagBlocksLowerTriangular" | custom-call | tf_op jit(solution)/shard_map/jit(cholesky)/cholesky | solution.py:73
  381.8 12.1 %cholesky.243 = f32[128,128]{1,0:T(8,128)S(1)} custom-call(f32[128,128]{1,0:T(8,128)S(1)} %cholesky.581), custom_call_target="Cholesky" | custom-call | tf_op jit(solution)/shard_map/jit(cholesky)/cholesky | solution.py:73
  394.5 9.8 %custom-call.67 = f32[1,128,128]{1,2,0:T(8,128)S(1)} custom-call(f32[1,128,128]{2,1,0:T(8,128)S(1)} %get-tuple-element.39), custom_call_target="InvertDiagBlocksLowerTriangular" | custom-call | tf_op jit(solution)/shard_map/jit(cholesky)/cholesky | solution.py:73
  407.7 11.7 %cholesky.466 = f32[128,128]{1,0:T(8,128)S(1)} custom-call(f32[128,128]{1,0:T(8,128)S(1)} %cholesky.586), custom_call_target="Cholesky" | custom-call | tf_op jit(solution)/shard_map/jit(cholesky)/cholesky | solution.py:73
  420.0 9.8 %custom-call.68 = f32[1,128,128]{1,2,0:T(8,128)S(1)} custom-call(f32[1,128,128]{2,1,0:T(8,128)S(1)} %get-tuple-element.36), custom_call_target="InvertDiagBlocksLowerTriangular" | custom-call | tf_op jit(solution)/shard_map/jit(cholesky)/cholesky | solution.py:73
  433.4 11.9 %cholesky.485 = f32[128,128]{1,0:T(8,128)S(1)} custom-call(f32[128,128]{1,0:T(8,128)S(1)} %cholesky.591), custom_call_target="Cholesky" | custom-call | tf_op jit(solution)/shard_map/jit(cholesky)/cholesky | solution.py:73
  445.9 9.8 %custom-call.69 = f32[1,128,128]{1,2,0:T(8,128)S(1)} custom-call(f32[1,128,128]{2,1,0:T(8,128)S(1)} %get-tuple-element.33), custom_call_target="InvertDiagBlocksLowerTriangular" | custom-call | tf_op jit(solution)/shard_map/jit(cholesky)/cholesky | solution.py:73
  459.1 11.7 %cholesky.504 = f32[128,128]{1,0:T(8,128)S(1)} custom-call(f32[128,128]{1,0:T(8,128)S(1)} %cholesky.596), custom_call_target="Cholesky" | custom-call | tf_op jit(solution)/shard_map/jit(cholesky)/cholesky | solution.py:73
  471.5 10.0 %custom-call.70 = f32[1,128,128]{1,2,0:T(8,128)S(1)} custom-call(f32[1,128,128]{2,1,0:T(8,128)S(1)} %get-tuple-element.30), custom_call_target="InvertDiagBlocksLowerTriangular" | custom-call | tf_op jit(solution)/shard_map/jit(cholesky)/cholesky | solution.py:73
  484.8 11.7 %cholesky.524 = f32[128,128]{1,0:T(8,128)S(1)} custom-call(f32[128,128]{1,0:T(8,128)S(1)} %cholesky.601), custom_call_target="Cholesky" | custom-call | tf_op jit(solution)/shard_map/jit(cholesky)/cholesky | solution.py:73
  497.2 9.8 %custom-call.71 = f32[1,128,128]{1,2,0:T(8,128)S(1)} custom-call(f32[1,128,128]{2,1,0:T(8,128)S(1)} %get-tuple-element.27), custom_call_target="InvertDiagBlocksLowerTriangular" | custom-call | tf_op jit(solution)/shard_map/jit(cholesky)/cholesky | solution.py:73
  510.0 12.1 %cholesky.544 = f32[128,128]{1,0:T(8,128)S(1)} custom-call(f32[128,128]{1,0:T(8,128)S(1)} %cholesky.606), custom_call_target="Cholesky" | custom-call | tf_op jit(solution)/shard_map/jit(cholesky)/cholesky | solution.py:73
  535.1 11.7 %cholesky.562 = f32[128,128]{1,0:T(8,128)S(1)} custom-call(f32[128,128]{1,0:T(8,128)S(1)} %convolution_subtract_fusion.6), custom_call_target="Cholesky" | custom-call | tf_op jit(solution)/shard_map/jit(cholesky)/cholesky | solution.py:73
  562.5 23.0 %while.1 = (s32[]{:T(128)}, f32[1024,1024]{1,0:T(8,128)}, s32[8,2]{0,1:T(2,128)S(1)}, f32[8,128,128]{2,1,0:T(8,128)S(1)}, s32[]{:T(128)}) while((s32[]{:T(128)}, f32[1024,1024]{1,0:T(8,128)}, s32[8,2]{0,1:T(2,128)S(1)}, f32[8,128,128]{2,1,0:T(8,128)S(1)}, s32[]{:T(128)}) %tuple.63), condition=%wide.while_cond, body=%wide.while_body.sunk | while | flops 2 | bytes 131189 | solution.py:74
  585.5 78.8 %custom-call.73 = f32[8,128,128]{1,2,0:T(8,128)S(1)} custom-call(f32[8,128,128]{2,1,0:T(8,128)S(1)} %get-tuple-element.10), custom_call_target="InvertDiagBlocksLowerTriangular" | custom-call | tf_op jit(solution)/shard_map/jit(_cho_solve)/triangular_solve | solution.py:74
  691.4 39.1 %psum.15 = f32[4]{0:T(128)S(1)} all-reduce(f32[4]{0:T(128)S(1)} %subtract_reduce_fusion), channel_id=1, replica_groups=mesh['rows'=32] {'rows'}, use_global_device_ids=true, to_apply=%region_19.20 | all-reduce | flops 4 | bytes 32 | tf_op jit(solution)/shard_map/psum | solution.py:79
  (168 shorter events, 152.1 us)
Async XLA Ops:
  7.2 262.6 %reduce-scatter.2.cloned.1.call-start = ((), (), s32[]{:S(2)}) async-start(), calls=%async_computation.1 | async-start | bytes 8650752 | tf_op jit(solution)/shard_map/reduce_scatter | solution.py:63
  9.4 5.7 copy-start.4
  9.4 5.7 copy-start.7
  93.4 17.5 %copy-start.3 = (s32[2048]{0:T(1024)S(1)}, s32[2048]{0:T(1024)}, u32[]{:S(2)}) copy-start(s32[2048]{0:T(1024)} %param.10) | copy-start | bytes 24580
  116.9 213.2 %all-gather.2.cloned.1.call-start = ((), (), s32[]{:S(2)}) async-start(), calls=%async_computation.2 | async-start | bytes 4325376 | tf_op jit(solution)/shard_map/all_gather | solution.py:70
  271.5 41.7 %copy-start.5 = (f32[1024]{0:T(1024)S(1)}, f32[1024]{0:T(1024)}, u32[]{:S(2)}) copy-start(f32[1024]{0:T(1024)} %param.7) | copy-start | bytes 12292
  313.1 359.9 %copy-start.2 = (f32[1024]{0:T(1024)}, f32[1024]{0:T(1024)S(1)}, u32[]{:S(2)}) copy-start(f32[1024]{0:T(1024)S(1)} %multiply_add_fusion) | copy-start | bytes 12292
  337.7 1.9 copy-start
  351.8 1.9 copy-start.1
  685.2 6.0 copy-start.6
  685.3 5.7 copy-start.8
Sparse Core Ops, SparseCore 0:
  117.0 152.7 reduce-scatter.1
  272.6 57.4 all-gather.1
where the time goes:
time: 745 us; the launch traced here: 738 us
  other arithmetic  282 us (38%)
  waiting for transfers between devices  170 us (23%)
  matrix products  127 us (17%)
  blocking collectives  76.2 us (10%)
  local copies, waits for them, and re-layouts  63 us (8%)
  between operations  19.6 us (3%)
    another operation x31, other arithmetic, body(): cholesky_factor = jnp.linalg.cholesky(hessian)  173 us
    reduce_scatter x1, waiting for transfers between devices, body(): lax.psum_scatter(jnp.take(mixed, local_rows, axis=0) * coefs[:, None], 'r...  153 us
    another operation x3, other arithmetic, body(): newton_step = jax.scipy.linalg.cho_solve((cholesky_factor, True), gradient)  83.6 us
    dot_general x1, matrix products, local_transform(): jnp.einsum('bx,axd->abd', low_matrix, first.reshape(high_order, low_order...  48.2 us
    psum x1, blocking collectives, body(): loss_total = lax.psum(jnp.sum(row_loss, axis=1), 'rows')  39.1 us
    psum x1, blocking collectives, body(): gradient = lax.psum(grad_part, 'rows') / total_rows + ridge * weights  37.1 us
    another operation x14, matrix products, body(): cholesky_factor = jnp.linalg.cholesky(hessian)  23.1 us
    another operation x24, local copies, waits for them, and re-layouts  22.8 us
  transfers between devices with their start and end apart: 2, of which 2 were waited for; matrix products, arithmetic and copies ran while one was open for 1% of the time, Pallas kernels for 0%

commit v1 on v0

v1 whole, which is shorter than its diff:
```python
import functools

import jax
import jax.numpy as jnp
from jax import lax
from jax.experimental import pallas as pl
from jax.experimental.pallas import tpu as pltpu
from jax.sharding import PartitionSpec as P

ridge = 0.05
LANES = 128
MESH = pl.DeviceIdType.MESH


def parity_sign(bits):
    for shift in (16, 8, 4, 2, 1):
        bits = bits ^ (bits >> shift)
    return (1 - 2 * (bits & 1)).astype(jnp.float32)


def sampled_kernel(rows_here, picks_ref, scaled_ref, out_ref, matrix):
    me = lax.axis_index("rows")
    picks = picks_ref[...]
    tile = picks.shape[0]
    lane = lax.broadcasted_iota(jnp.int32, (tile, LANES), 1)
    chunks = rows_here // LANES
    local = picks & (rows_here - 1)
    owner_sign = parity_sign((picks >> (rows_here.bit_length() - 1)) & me)
    low = parity_sign(local & lane) * owner_sign
    high = parity_sign((local >> 7) & lane)
    for chunk in range(chunks):
        matrix[:, chunk * LANES : (chunk + 1) * LANES] = (
            low * high[:, chunk : chunk + 1]
        ).astype(jnp.bfloat16)
    out_ref[...] = jnp.dot(
        matrix[...], scaled_ref[...], preferred_element_type=jnp.float32
    )


def sampled_transform(picks, scaled):
    rows_here, width = scaled.shape
    total = picks.shape[0]
    tile = 256
    return pl.pallas_call(
        functools.partial(sampled_kernel, rows_here),
        grid=(total // tile,),
        out_shape=jax.ShapeDtypeStruct((total, width), jnp.float32),
        in_specs=[
            pl.BlockSpec((tile, 1), lambda i: (i, 0)),
            pl.BlockSpec((rows_here, width), lambda i: (0, 0)),
        ],
        out_specs=pl.BlockSpec((tile, width), lambda i: (i, 0)),
        scratch_shapes=[pltpu.VMEM((tile, rows_here), jnp.bfloat16)],
        name="sampled_transform",
    )(picks.reshape(total, 1), scaled)


def allsum_kernel(count, own_ref, out_ref, slots, send_sem, recv_sem):
    me = lax.axis_index("rows")
    barrier = pltpu.get_barrier_semaphore()

    @pl.loop(1, count)
    def greet(step):
        pl.semaphore_signal(
            barrier, inc=1, device_id=(lax.rem(me + step, count),), device_id_type=MESH
        )

    pl.semaphore_wait(barrier, count - 1)

    def copy(step):
        return pltpu.make_async_remote_copy(
            src_ref=own_ref,
            dst_ref=slots.at[me],
            send_sem=send_sem.at[step],
            recv_sem=recv_sem.at[step],
            device_id=(lax.rem(me + step, count),),
            device_id_type=MESH,
        )

    @pl.loop(1, count)
    def send(step):
        copy(step).start()

    slots[me] = own_ref[...]

    @pl.loop(1, count)
    def finish(step):
        copy(step).wait()

    out_ref[...] = jnp.sum(slots[...], axis=0)


def allsum(own, count, ident):
    return pl.pallas_call(
        functools.partial(allsum_kernel, count),
        out_shape=jax.ShapeDtypeStruct(own.shape, jnp.float32),
        in_specs=[pl.BlockSpec(memory_space=pltpu.VMEM)],
        out_specs=pl.BlockSpec(memory_space=pltpu.VMEM),
        scratch_shapes=[
            pltpu.VMEM((count,) + own.shape, jnp.float32),
            pltpu.SemaphoreType.DMA((count,)),
            pltpu.SemaphoreType.DMA((count,)),
        ],
        compiler_params=pltpu.CompilerParams(collective_id=ident, has_side_effects=True),
        name="allsum_%d" % ident,
    )(own)


def solve_kernel(total_rows, piece_ref, gradient_ref, step_ref, hess, vec_r, vec_p, vec_q):
    width = piece_ref.shape[1]
    block = 256
    scale = 1.0 / total_rows
    for start in range(0, width, block):
        gram = lax.dot_general(
            piece_ref[:, start : start + block],
            piece_ref[...],
            (((0,), (0,)), ((), ())),
            preferred_element_type=jnp.float32,
        )
        row = lax.broadcasted_iota(jnp.int32, (block, width), 0) + start
        col = lax.broadcasted_iota(jnp.int32, (block, width), 1)
        hess[start : start + block, :] = gram * scale + jnp.where(row == col, ridge, 0.0)
    diag = jnp.zeros((1, width), jnp.float32)
    for start in range(0, width, block):
        row = lax.broadcasted_iota(jnp.int32, (block, width), 0) + start
        col = lax.broadcasted_iota(jnp.int32, (block, width), 1)
        diag = diag + jnp.sum(
            jnp.where(row == col, hess[start : start + block, :], 0.0), axis=0, keepdims=True
        )
    inverse = 1.0 / diag
    right = gradient_ref[...]
    vec_r[...] = right
    start_z = right * inverse
    vec_p[...] = start_z
    step_ref[...] = jnp.zeros_like(right)
    start_rz = jnp.sum(right * start_z, axis=1, keepdims=True)
    goal = jnp.max(start_rz) * 1e-13

    def product():
        tiles = width // LANES
        sums = [jnp.zeros((8, LANES), jnp.float32) for tile in range(tiles)]
        for piece in range(tiles):
            span = slice(piece * LANES, (piece + 1) * LANES)
            column = jnp.broadcast_to(vec_p[:, span], (LANES, LANES)).T
            for tile in range(tiles):
                prod = hess[span, tile * LANES : (tile + 1) * LANES] * column
                sums[tile] = sums[tile] + jnp.sum(prod.reshape(LANES // 8, 8, LANES), axis=0)
        for tile in range(tiles):
            vec_q[:, tile * LANES : (tile + 1) * LANES] = jnp.sum(
                sums[tile], axis=0, keepdims=True
            )

    def go(carry):
        done, level, rz = carry
        return jnp.logical_and(level > goal, done < 8 * width)

    def advance(carry):
        done, level, rz = carry
        product()
        direction, image = vec_p[...], vec_q[...]
        curve = jnp.sum(direction * image, axis=1, keepdims=True)
        alpha = jnp.where(curve > 0.0, rz / curve, 0.0)
        step_ref[...] = step_ref[...] + alpha * direction
        rest = vec_r[...] - alpha * image
        vec_r[...] = rest
        scaled_rest = rest * inverse
        next_rz = jnp.sum(rest * scaled_rest, axis=1, keepdims=True)
        beta = jnp.where(rz > 0.0, next_rz / rz, 0.0)
        vec_p[...] = scaled_rest + beta * direction
        return done + 1, jnp.max(next_rz), next_rz

    lax.while_loop(go, advance, (jnp.int32(0), jnp.max(start_rz), start_rz))


def newton_solve(piece, gradient, total_rows):
    width = piece.shape[1]
    vector = pltpu.VMEM((1, width), jnp.float32)
    return pl.pallas_call(
        functools.partial(solve_kernel, total_rows),
        out_shape=jax.ShapeDtypeStruct((1, width), jnp.float32),
        in_specs=[pl.BlockSpec(memory_space=pltpu.VMEM)] * 2,
        out_specs=pl.BlockSpec(memory_space=pltpu.VMEM),
        scratch_shapes=[pltpu.VMEM((width, width), jnp.float32), vector, vector, vector],
        name="newton_solve",
    )(piece, gradient.reshape(1, width)).reshape(width)


def body(design, weights, labels, signs, sample_rows):
    rows_here, width = design.shape
    device_count = lax.axis_size("rows")
    total_rows = rows_here * device_count
    margins = jnp.dot(design, weights.astype(jnp.bfloat16), preferred_element_type=jnp.float32)
    prob = jax.nn.sigmoid(margins)
    target = labels.astype(jnp.float32)
    misfit = (prob - target).astype(jnp.bfloat16)
    grad_part = jnp.dot(misfit, design, preferred_element_type=jnp.float32)
    factor_rows = (1.0 - 2.0 * signs.astype(jnp.float32)) * jnp.sqrt(prob * (1.0 - prob))
    scaled = (design * factor_rows[:, None]).astype(jnp.bfloat16)
    grad_sum = allsum(grad_part.reshape(width // LANES, LANES), device_count, 0)
    gradient = grad_sum.reshape(width) / total_rows + ridge * weights
    norm_factor = 1.0 / jnp.sqrt(jnp.float32(sample_rows.shape[0]))
    own_part = sampled_transform(sample_rows, scaled)
    sketch_own = lax.psum_scatter(own_part, "rows", scatter_dimension=0, tiled=True)
    sketch_low = (sketch_own * norm_factor).astype(jnp.bfloat16)
    piece = lax.all_gather(sketch_low, "rows", axis=0, tiled=True)
    newton_step = newton_solve(piece, gradient, total_rows)
    along = jnp.dot(design, newton_step.astype(jnp.bfloat16), preferred_element_type=jnp.float32)
    lengths = jnp.array([1.0, 0.5, 0.25, 0.125], jnp.float32)
    trial = margins[None, :] - lengths[:, None] * along[None, :]
    row_loss = jnp.logaddexp(0.0, trial) - target[None, :] * trial
    loss_part = jnp.sum(row_loss, axis=1)
    loss_tile = jnp.broadcast_to(jnp.pad(loss_part, (0, 4))[:, None], (8, LANES))
    loss_total = allsum(loss_tile, device_count, 1)[:4, 0]
    moved = weights[None, :] - lengths[:, None] * newton_step[None, :]
    losses = loss_total / total_rows + 0.5 * ridge * jnp.sum(moved * moved, axis=1)
    return (gradient, newton_step, losses)


def solution(mesh):
    placed = (P("rows", None), P(), P("rows"), P("rows"), P())
    return jax.shard_map(
        body, mesh=mesh, in_specs=placed, out_specs=(P(), P(), P()), check_vma=False
    )
```

time: 745 us -> 321 us (0.43)
  other arithmetic: 282 us -> 14.2 us
  matrix products: 127 us -> 16.5 us
  blocking collectives: 76.2 us -> 0 us
  Pallas kernels: 0 us -> 76.1 us
  local copies, waits for them, and re-layouts: 63 us -> 2.08 us
  waiting for transfers between devices: 170 us -> 196 us
    another operation x34 -> x0, other arithmetic: 257 us -> none  [the longest x31 173 us: body(): cholesky_factor = jnp.linalg.cholesky(hessian)]
    psum x2 -> x0, blocking collectives: 76.2 us -> none  [the longest x1 39.1 us: body(): loss_total = lax.psum(jnp.sum(row_loss, axis=1), 'rows')]
    pallas_call x0 -> x4, Pallas kernels: none -> 76.1 us  [the longest x1 32.7 us: sampled_transform(): pl.pallas_call(functools.partial(sampled_kernel, rows_here), grid=(total...]
    dot_general x3 -> x0, matrix products: 67.3 us -> none  [the longest x1 48.2 us: local_transform(): jnp.einsum('bx,axd->abd', low_matrix, first.reshape(high_order, low_order...]
    another operation x44 -> x0, matrix products: 43.6 us -> none  [the longest x14 23.1 us: body(): cholesky_factor = jnp.linalg.cholesky(hessian)]
    all_gather x1, waiting for transfers between devices: 17 us -> 43.4 us  [body(): piece = lax.all_gather(sketch_low, 'rows', axis=0, tiled=True)]
    another operation x37 -> x0, local copies, waits for them, and re-layouts: 25.4 us -> none
    gather x1 -> x0, local copies, waits for them, and re-layouts: 17.5 us -> none  [body(): jnp.take(mixed, local_rows, axis=0) * coefs[:, None]]
  transfers between devices with their start and end apart: 2 -> 2, of which waited for: 2 -> 2; matrix products, arithmetic and copies ran while one was open for 1% -> 2% of each run, Pallas kernels for 0% -> 3%
where the time goes in v1:
time: 321 us; the launch traced here: 319 us
  waiting for transfers between devices  196 us (61%)
  Pallas kernels  76.1 us (24%)
  matrix products  16.5 us (5%)
  other arithmetic  14.2 us (4%)
  between operations  14.1 us (4%)
    reduce_scatter x1, waiting for transfers between devices, body(): lax.psum_scatter(own_part, 'rows', scatter_dimension=0, tiled=True)  153 us
    all_gather x1, waiting for transfers between devices, body(): piece = lax.all_gather(sketch_low, 'rows', axis=0, tiled=True)  43.4 us
    pallas_call x1, Pallas kernels, sampled_transform(): pl.pallas_call(functools.partial(sampled_kernel, rows_here), grid=(total...  32.7 us
    pallas_call x1, Pallas kernels, newton_solve(): pl.pallas_call(functools.partial(solve_kernel, total_rows), out_shape=jax...  24.3 us
    pallas_call x2, Pallas kernels, allsum(): pl.pallas_call(functools.partial(allsum_kernel, count), out_shape=jax.Sha...  19 us
    convert_element_type x1, other arithmetic, body(): scaled = (design * factor_rows[:, None]).astype(jnp.bfloat16)  8.02 us
  transfers between devices with their start and end apart: 2, of which 2 were waited for; matrix products, arithmetic and copies ran while one was open for 2% of the time, Pallas kernels for 3%

profile of v1, /device:TPU:0, one launch (start us, length us, event | category | flops | bytes accessed | tf_op | source)
XLA Modules:
  0.0 319.4 jit_solution(14464246603258359602)
XLA Ops:
  7.2 0.0 reduce-scatter.2.cloned.1.call-start
  7.2 0.7 convert_element_type.26
  7.9 5.6 %fusion.4 = f32[1,4096]{1,0:T(1,128)S(1)} fusion(bf16[4096,1024]{1,0:T(8,128)(2,1)} %param.6, bf16[1024,1]{0,1:T(2,128)(2,1)S(1)} %reshape.34), kind=kOutput, calls=%fused_computation.15 | convolution fusion | flops 8388608 | bytes 8407040 | tf_op jit(solution)/shard_map/dot_general | solution.py:192
  13.6 8.0 %multiply_convert_fusion.scaled_ref = bf16[4096,1024]{1,0:T(8,128)(2,1)} fusion(bf16[4096,1024]{1,0:T(8,128)(2,1)} %param.6, f32[4096]{0:T(1024)S(1)} %get-tuple-element.3), kind=kLoop, calls=%fused_computation | loop fusion | flops 12582912 | bytes 16793600 | tf_op jit(solution)/shard_map/convert_element_type | solution.py:198
  21.7 1.4 copy.10.picks_ref
  23.0 32.7 %sampled_transform.1 = f32[2048,1024]{1,0:T(8,128)} custom-call(s32[2048,1]{1,0:T(8,128)} %copy.10.picks_ref, bf16[4096,1024]{1,0:T(8,128)(2,1)} %multiply_convert_fusion.scaled_ref), custom_call_target="tpu_custom_call" | custom-call | tf_op jit(solution)/shard_map/sampled_transform/pallas_call | solution.py:44
  55.7 0.0 reduce-scatter.2.cloned.1.call-update
  55.8 0.0 all-gather.2.cloned.1.call-start
  55.8 153.0 %reduce-scatter.2.cloned.1.call-done = f32[64,1024]{1,0:T(8,128)} async-done(((f32[2048,1024]{1,0:T(8,128)}), f32[64,1024]{1,0:T(8,128)}) %reduce-scatter.2.cloned.1.call-update) | async-done | bytes 262160 | tf_op jit(solution)/shard_map/reduce_scatter | solution.py:203
  208.8 1.6 multiply_convert_fusion.1
  210.4 0.0 all-gather.2.cloned.1.call-update
  210.5 5.2 %fusion.5 = f32[1,1024]{1,0:T(1,128)} fusion(bf16[4096,1]{0,1:T(2,128)(2,1)S(1)} %reshape.36, bf16[4096,1024]{1,0:T(8,128)(2,1)} %param.6), kind=kOutput, calls=%fused_computation.16 | convolution fusion | flops 8388608 | bytes 8400896 | tf_op jit(solution)/shard_map/dot_general | solution.py:196
  215.6 9.5 %allsum_0.1 = f32[8,128]{1,0:T(8,128)} custom-call(f32[8,128]{1,0:T(8,128)} %bitcast.23), custom_call_target="tpu_custom_call" | custom-call | tf_op jit(solution)/shard_map/allsum_0/pallas_call | solution.py:94
  225.1 1.3 bitcast_add_fusion
  226.4 43.4 %all-gather.2.cloned.1.call-done.piece_ref = bf16[2048,1024]{1,0:T(8,128)(2,1)} async-done(((bf16[64,1024]{1,0:T(8,128)(2,1)}), bf16[2048,1024]{1,0:T(8,128)(2,1)}) %all-gather.2.cloned.1.call-update) | async-done | bytes 4194320 | tf_op jit(solution)/shard_map/all_gather | solution.py:205
  269.8 24.3 %newton_solve.1 = f32[1,1024]{1,0:T(1,128)} custom-call(bf16[2048,1024]{1,0:T(8,128)(2,1)} %all-gather.2.cloned.1.call-done.piece_ref, f32[1,1024]{1,0:T(1,128)} %bitcast.22), custom_call_target="tpu_custom_call" | custom-call | tf_op jit(solution)/shard_map/newton_solve/pallas_call | solution.py:178
  294.1 0.8 convert_element_type.33
  294.9 5.6 %fusion.6 = f32[1,4096]{1,0:T(1,128)S(1)} fusion(bf16[1024,1]{0,1:T(2,128)(2,1)S(1)} %reshape.38, bf16[4096,1024]{1,0:T(8,128)(2,1)} %param.6), kind=kOutput, calls=%fused_computation.17 | convolution fusion | flops 8388608 | bytes 8407040 | tf_op jit(solution)/shard_map/dot_general | solution.py:207
  300.5 0.2 multiply_reduce_fusion
  300.7 0.3 subtract_reduce_fusion
  301.0 0.7 broadcast_in_dim.2.own_ref
  301.7 9.6 %allsum_1.1 = f32[8,128]{1,0:T(8,128)} custom-call(f32[8,128]{1,0:T(8,128)} %broadcast_in_dim.2.own_ref), custom_call_target="tpu_custom_call" | custom-call | tf_op jit(solution)/shard_map/allsum_1/pallas_call | solution.py:94
  311.3 0.8 multiply_reduce_fusion.1
  312.1 0.5 multiply_add_fusion
  (18 shorter events, 0.1 us)
Async XLA Ops:
  7.2 6.4 %copy-start = (s32[4096]{0:T(1024)S(1)}, s32[4096]{0:T(1024)}, u32[]{:S(2)}) copy-start(s32[4096]{0:T(1024)} %param.8) | copy-start | bytes 49156
  7.2 6.4 %copy-start.3 = (s32[4096]{0:T(1024)S(1)}, s32[4096]{0:T(1024)}, u32[]{:S(2)}) copy-start(s32[4096]{0:T(1024)} %param.9) | copy-start | bytes 49156
  7.2 201.6 %reduce-scatter.2.cloned.1.call-start = ((), (), s32[]{:S(2)}) async-start(), calls=%async_computation.1 | async-start | bytes 8650752 | tf_op jit(solution)/shard_map/reduce_scatter | solution.py:203
  13.6 8.0 %copy-start.4 = (s32[2048]{0:T(1024)S(1)}, s32[2048]{0:T(1024)}, u32[]{:S(2)}) copy-start(s32[2048]{0:T(1024)} %param.10) | copy-start | bytes 24580
  55.8 169.3 %copy-start.1 = (f32[1024]{0:T(1024)S(1)}, f32[1024]{0:T(1024)}, u32[]{:S(2)}) copy-start(f32[1024]{0:T(1024)} %param.7) | copy-start | bytes 12292
  55.8 214.0 %all-gather.2.cloned.1.call-start = ((), (), s32[]{:S(2)}) async-start(), calls=%async_computation.2 | async-start | bytes 4325376 | tf_op jit(solution)/shard_map/all_gather | solution.py:205
  215.6 84.9 %copy-start.5 = (f32[4]{0:T(128)S(1)}, f32[4]{0:T(128)}, u32[]{:S(2)}) copy-start(f32[4]{0:T(128)} %constant.22.clone) | copy-start | bytes 52
  294.1 6.4 %copy-start.2 = (f32[1,1024]{1,0:T(1,128)S(1)}, f32[1,1024]{1,0:T(1,128)}, u32[]{:S(2)}) copy-start(f32[1,1024]{1,0:T(1,128)} %newton_solve.1) | copy-start | bytes 12292
Sparse Core Ops, SparseCore 0:
  55.9 152.8 reduce-scatter.1
  211.6 58.1 all-gather.1

commit v2 on v1

--- a/solution.py
+++ b/solution.py
@@ -1,4 +1,5 @@
 import functools
+import math
 
 import jax
 import jax.numpy as jnp
@@ -106,6 +107,173 @@
     )(own)
 
 
+def exchange_kernel(
+    orders, spans, part_ref, grad_ref, sketch_ref, gsum_ref,
+    total, arrive_first, arrive_rest, grad_slots, grad_own,
+    send_sem, recv_sem, back_send, back_recv, grad_send, grad_recv,
+):
+    me = lax.axis_index("rows")
+    steps = len(orders[0])
+    rows = part_ref.shape[0]
+    norm = 1.0 / math.sqrt(rows)
+    half = rows // 2
+    groups = range(len(orders))
+
+    def peer(bit):
+        return me ^ (1 << bit)
+
+    def mine(bit):
+        return (me >> bit) & 1
+
+    barrier = pltpu.get_barrier_semaphore()
+    for bit in range(steps):
+        pl.semaphore_signal(barrier, inc=1, device_id=(peer(bit),), device_id_type=MESH)
+    pl.semaphore_wait(barrier, steps)
+
+    def remote(source, target, out_sem, in_sem, bit):
+        return pltpu.make_async_remote_copy(
+            src_ref=source, dst_ref=target, send_sem=out_sem, recv_sem=in_sem,
+            device_id=(peer(bit),), device_id_type=MESH,
+        )
+
+    core = orders[0][0]
+    base = pl.multiple_of(mine(core) * half, half)
+    other = pl.multiple_of((1 - mine(core)) * half, half)
+    sent = []
+    pending = {}
+
+    def start(copy, key):
+        copy.start()
+        sent.append(copy)
+        pending[key] = copy
+
+    def grad_start(step):
+        source = grad_ref if step == 0 else grad_own.at[step - 1]
+        start(
+            remote(source, grad_slots.at[step], grad_send.at[step], grad_recv.at[step], step),
+            ("grad", step),
+        )
+
+    def grad_finish(step):
+        pending[("grad", step)].wait_recv()
+        before = grad_ref[...] if step == 0 else grad_own[step - 1]
+        grad_own[step] = before + grad_slots[step]
+
+    grad_start(0)
+    for group in groups:
+        cols = slice(*spans[group])
+        start(
+            remote(
+                part_ref.at[pl.ds(other, half), cols], arrive_first.at[:, cols],
+                send_sem.at[0, group], recv_sem.at[0, group], core,
+            ),
+            (0, group),
+        )
+
+    offsets = [0 for group in groups]
+    history = [[] for group in groups]
+
+    def rest_start(step, group):
+        cols = slice(*spans[group])
+        size = half >> step
+        bit = orders[group][step]
+        place = half - (half >> (step - 1))
+        history[group].append(offsets[group])
+        away = pl.multiple_of(offsets[group] + (1 - mine(bit)) * size, size)
+        start(
+            remote(
+                total.at[pl.ds(away, size), cols], arrive_rest.at[pl.ds(place, size), cols],
+                send_sem.at[step, group], recv_sem.at[step, group], bit,
+            ),
+            (step, group),
+        )
+        offsets[group] = pl.multiple_of(offsets[group] + mine(bit) * size, size)
+
+    for step in range(steps):
+        if step > 0:
+            grad_start(step)
+        for group in groups:
+            cols = slice(*spans[group])
+            pending[(step, group)].wait_recv()
+            if step == 0:
+                total[:, cols] = part_ref[pl.ds(base, half), cols] + arrive_first[:, cols]
+            else:
+                size = half >> step
+                place = half - (half >> (step - 1))
+                keep = pl.ds(offsets[group], size)
+                total[keep, cols] = total[keep, cols] + arrive_rest[place : place + size, cols]
+            if step + 1 < steps:
+                rest_start(step + 1, group)
+        grad_finish(step)
+
+    def back_start(step, group):
+        cols = slice(*spans[group])
+        bit = orders[group][step]
+        size = half >> step
+        place = pl.ds(pl.multiple_of(base + offsets[group], size), size)
+        start(
+            remote(
+                sketch_ref.at[place, cols], sketch_ref.at[place, cols],
+                back_send.at[step, group], back_recv.at[step, group], bit,
+            ),
+            ("back", step, group),
+        )
+
+    last = half >> (steps - 1)
+    for group in groups:
+        cols = slice(*spans[group])
+        place = pl.ds(pl.multiple_of(base + offsets[group], last), last)
+        sketch_ref[place, cols] = (total[pl.ds(offsets[group], last), cols] * norm).astype(
+            sketch_ref.dtype
+        )
+        back_start(steps - 1, group)
+    for step in range(steps - 1, -1, -1):
+        for group in groups:
+            pending[("back", step, group)].wait_recv()
+            if step > 0:
+                offsets[group] = history[group][step - 1]
+                back_start(step - 1, group)
+    gsum_ref[...] = grad_own[steps - 1]
+    for copy in sent:
+        copy.wait_send()
+
+
+def exchange(part, grad, count):
+    rows, width = part.shape
+    bits = count.bit_length() - 1
+    rest = list(range(1, bits))
+    tiles = width // LANES
+    lanes = 3
+    cuts = [-(-tiles * group // lanes) * LANES for group in range(lanes + 1)]
+    spans = [(cuts[group], cuts[group + 1]) for group in range(lanes)]
+    orders = []
+    for group in range(lanes):
+        turn = group * len(rest) // lanes
+        orders.append([0] + rest[turn:] + rest[:turn])
+    grid_sem = pltpu.SemaphoreType.DMA((bits, lanes))
+    line_sem = pltpu.SemaphoreType.DMA((bits,))
+    vmem = pl.BlockSpec(memory_space=pltpu.VMEM)
+    return pl.pallas_call(
+        functools.partial(exchange_kernel, orders, spans),
+        out_shape=(
+            jax.ShapeDtypeStruct((rows, width), jnp.bfloat16),
+            jax.ShapeDtypeStruct(grad.shape, jnp.float32),
+        ),
+        in_specs=[vmem, vmem],
+        out_specs=(vmem, vmem),
+        scratch_shapes=[
+            pltpu.VMEM((rows // 2, width), jnp.float32),
+            pltpu.VMEM((rows // 2, width), jnp.float32),
+            pltpu.VMEM((rows // 2, width), jnp.float32),
+            pltpu.VMEM((bits,) + grad.shape, jnp.float32),
+            pltpu.VMEM((bits,) + grad.shape, jnp.float32),
+            grid_sem, grid_sem, grid_sem, grid_sem, line_sem, line_sem,
+        ],
+        compiler_params=pltpu.CompilerParams(collective_id=2, has_side_effects=True),
+        name="exchange",
+    )(part, grad)
+
+
 def solve_kernel(total_rows, piece_ref, gradient_ref, step_ref, hess, vec_r, vec_p, vec_q):
     width = piece_ref.shape[1]
     block = 256
@@ -196,13 +364,11 @@
     grad_part = jnp.dot(misfit, design, preferred_element_type=jnp.float32)
     factor_rows = (1.0 - 2.0 * signs.astype(jnp.float32)) * jnp.sqrt(prob * (1.0 - prob))
     scaled = (design * factor_rows[:, None]).astype(jnp.bfloat16)
-    grad_sum = allsum(grad_part.reshape(width // LANES, LANES), device_count, 0)
+    own_part = sampled_transform(sample_rows, scaled)
+    piece, grad_sum = exchange(
+        own_part, grad_part.reshape(width // LANES, LANES), device_count
+    )
     gradient = grad_sum.reshape(width) / total_rows + ridge * weights
-    norm_factor = 1.0 / jnp.sqrt(jnp.float32(sample_rows.shape[0]))
-    own_part = sampled_transform(sample_rows, scaled)
-    sketch_own = lax.psum_scatter(own_part, "rows", scatter_dimension=0, tiled=True)
-    sketch_low = (sketch_own * norm_factor).astype(jnp.bfloat16)
-    piece = lax.all_gather(sketch_low, "rows", axis=0, tiled=True)
     newton_step = newton_solve(piece, gradient, total_rows)
     along = jnp.dot(design, newton_step.astype(jnp.bfloat16), preferred_element_type=jnp.float32)
     lengths = jnp.array([1.0, 0.5, 0.25, 0.125], jnp.float32)

time: 321 us -> 193 us (0.60)
  waiting for transfers between devices: 196 us -> 0 us
  Pallas kernels: 76.1 us -> 161 us
  between operations: 14.1 us -> 0.73 us
    reduce_scatter x1 -> x0, waiting for transfers between devices: 153 us -> none  [body(): lax.psum_scatter(own_part, 'rows', scatter_dimension=0, tiled=True)]
    pallas_call x0 -> x1, Pallas kernels: none -> 91.7 us  [exchange(): pl.pallas_call(functools.partial(exchange_kernel, orders, spans), out_sha...]
    all_gather x1 -> x0, waiting for transfers between devices: 43.4 us -> none  [body(): piece = lax.all_gather(sketch_low, 'rows', axis=0, tiled=True)]
    pallas_call x2 -> x1, Pallas kernels: 19 us -> 11 us  [allsum(): pl.pallas_call(functools.partial(allsum_kernel, count), out_shape=jax.Sha...]
  transfers between devices with their start and end apart: 2 -> 0, of which waited for: 2 -> 0; matrix products, arithmetic and copies ran while one was open for 2% -> 0% of each run, Pallas kernels for 3% -> 0%
where the time goes in v2:
time: 193 us
  Pallas kernels  161 us (83%)
  matrix products  16.5 us (9%)
  other arithmetic  12.6 us (7%)
  local copies, waits for them, and re-layouts  2.1 us (1%)
    pallas_call x1, Pallas kernels, exchange(): pl.pallas_call(functools.partial(exchange_kernel, orders, spans), out_sha...  91.7 us
    pallas_call x1, Pallas kernels, sampled_transform(): pl.pallas_call(functools.partial(sampled_kernel, rows_here), grid=(total...  32.7 us
    pallas_call x1, Pallas kernels, newton_solve(): pl.pallas_call(functools.partial(solve_kernel, total_rows), out_shape=jax...  25.3 us
    pallas_call x1, Pallas kernels, allsum(): pl.pallas_call(functools.partial(allsum_kernel, count), out_shape=jax.Sha...  11 us
    convert_element_type x1, other arithmetic, body(): scaled = (design * factor_rows[:, None]).astype(jnp.bfloat16)  8.01 us
    dot_general x1, matrix products, body(): jnp.dot(design, weights.astype(jnp.bfloat16), preferred_element_type=jnp....  5.64 us
    dot_general x1, matrix products, body(): jnp.dot(design, newton_step.astype(jnp.bfloat16), preferred_element_type=...  5.64 us
    dot_general x1, matrix products, body(): grad_part = jnp.dot(misfit, design, preferred_element_type=jnp.float32)  5.18 us

profile of v2, /device:TPU:0, one launch (start us, length us, event | category | flops | bytes accessed | tf_op | source)
XLA Modules:
  0.0 192.5 jit_solution(18291944398010894325)
XLA Ops:
  0.6 0.0 copy-start
  0.6 0.0 copy-start.3
  0.7 0.7 convert_element_type.25
  1.4 5.6 %fusion.4 = f32[1,4096]{1,0:T(1,128)S(1)} fusion(bf16[4096,1024]{1,0:T(8,128)(2,1)} %param.6, bf16[1024,1]{0,1:T(2,128)(2,1)S(1)} %reshape.34), kind=kOutput, calls=%fused_computation.14 | convolution fusion | flops 8388608 | bytes 8407040 | tf_op jit(solution)/shard_map/dot_general | solution.py:360
  7.0 0.0 copy-done
  7.1 0.0 copy-start.4
  7.1 8.0 %multiply_convert_fusion.scaled_ref = bf16[4096,1024]{1,0:T(8,128)(2,1)} fusion(bf16[4096,1024]{1,0:T(8,128)(2,1)} %param.6, f32[4096]{0:T(1024)S(1)} %get-tuple-element.8), kind=kLoop, calls=%fused_computation | loop fusion | flops 12582912 | bytes 16793600 | tf_op jit(solution)/shard_map/convert_element_type | solution.py:366
  15.1 1.4 copy.10.picks_ref
  16.5 32.7 %sampled_transform.1.part_ref = f32[2048,1024]{1,0:T(8,128)} custom-call(s32[2048,1]{1,0:T(8,128)} %copy.10.picks_ref, bf16[4096,1024]{1,0:T(8,128)(2,1)} %multiply_convert_fusion.scaled_ref), custom_call_target="tpu_custom_call" | custom-call | tf_op jit(solution)/shard_map/sampled_transform/pallas_call | solution.py:45
  49.2 0.0 copy-start.1
  49.2 5.2 %fusion.5 = f32[1,1024]{1,0:T(1,128)} fusion(bf16[4096,1]{0,1:T(2,128)(2,1)S(1)} %reshape.36, bf16[4096,1024]{1,0:T(8,128)(2,1)} %param.6), kind=kOutput, calls=%fused_computation.15 | convolution fusion | flops 8388608 | bytes 8400896 | tf_op jit(solution)/shard_map/dot_general | solution.py:364
  54.4 91.7 %exchange.1 = (bf16[2048,1024]{1,0:T(8,128)(2,1)}, f32[8,128]{1,0:T(8,128)}) custom-call(f32[2048,1024]{1,0:T(8,128)} %sampled_transform.1.part_ref, f32[8,128]{1,0:T(8,128)} %bitcast.23), custom_call_target="tpu_custom_call" | custom-call | tf_op jit(solution)/shard_map/exchange/pallas_call | solution.py:256
  146.1 0.0 copy-start.5
  146.1 1.3 bitcast_add_fusion
  147.4 25.3 %newton_solve.1 = f32[1,1024]{1,0:T(1,128)} custom-call(bf16[2048,1024]{1,0:T(8,128)(2,1)} %get-tuple-element.6.piece_ref, f32[1,1024]{1,0:T(1,128)} %bitcast.22), custom_call_target="tpu_custom_call" | custom-call | tf_op jit(solution)/shard_map/newton_solve/pallas_call | solution.py:346
  172.6 0.8 convert_element_type.29
  173.4 5.6 %fusion.6 = f32[1,4096]{1,0:T(1,128)S(1)} fusion(bf16[1024,1]{0,1:T(2,128)(2,1)S(1)} %reshape.38, bf16[4096,1024]{1,0:T(8,128)(2,1)} %param.6), kind=kOutput, calls=%fused_computation.16 | convolution fusion | flops 8388608 | bytes 8407040 | tf_op jit(solution)/shard_map/dot_general | solution.py:373
  179.1 0.3 subtract_reduce_fusion
  179.4 0.7 broadcast_in_dim.2.own_ref
  180.0 11.0 %allsum_1.1 = f32[8,128]{1,0:T(8,128)} custom-call(f32[8,128]{1,0:T(8,128)} %broadcast_in_dim.2.own_ref), custom_call_target="tpu_custom_call" | custom-call | tf_op jit(solution)/shard_map/allsum_1/pallas_call | solution.py:95
  191.0 0.8 multiply_reduce_fusion.1
  191.8 0.0 copy-done.2
  191.8 0.2 multiply_reduce_fusion
  192.0 0.5 multiply_add_fusion
  (11 shorter events, 0.1 us)
Async XLA Ops:
  0.6 6.4 %copy-start = (s32[4096]{0:T(1024)S(1)}, s32[4096]{0:T(1024)}, u32[]{:S(2)}) copy-start(s32[4096]{0:T(1024)} %param.8) | copy-start | bytes 49156
  0.6 6.4 %copy-start.3 = (s32[4096]{0:T(1024)S(1)}, s32[4096]{0:T(1024)}, u32[]{:S(2)}) copy-start(s32[4096]{0:T(1024)} %param.9) | copy-start | bytes 49156
  7.1 8.0 %copy-start.4 = (s32[2048]{0:T(1024)S(1)}, s32[2048]{0:T(1024)}, u32[]{:S(2)}) copy-start(s32[2048]{0:T(1024)} %param.10) | copy-start | bytes 24580
  49.2 96.9 %copy-start.1 = (f32[1024]{0:T(1024)S(1)}, f32[1024]{0:T(1024)}, u32[]{:S(2)}) copy-start(f32[1024]{0:T(1024)} %param.7) | copy-start | bytes 12292
  146.1 33.0 %copy-start.5 = (f32[4]{0:T(128)S(1)}, f32[4]{0:T(128)}, u32[]{:S(2)}) copy-start(f32[4]{0:T(128)} %constant.20.clone) | copy-start | bytes 52
  172.6 19.2 %copy-start.2 = (f32[1,1024]{1,0:T(1,128)S(1)}, f32[1,1024]{1,0:T(1,128)}, u32[]{:S(2)}) copy-start(f32[1,1024]{1,0:T(1,128)} %newton_solve.1) | copy-start | bytes 12292

commit v3 on v2

--- a/solution.py
+++ b/solution.py
@@ -19,41 +19,111 @@
     return (1 - 2 * (bits & 1)).astype(jnp.float32)
 
 
-def sampled_kernel(rows_here, picks_ref, scaled_ref, out_ref, matrix):
-    me = lax.axis_index("rows")
-    picks = picks_ref[...]
-    tile = picks.shape[0]
-    lane = lax.broadcasted_iota(jnp.int32, (tile, LANES), 1)
-    chunks = rows_here // LANES
-    local = picks & (rows_here - 1)
-    owner_sign = parity_sign((picks >> (rows_here.bit_length() - 1)) & me)
-    low = parity_sign(local & lane) * owner_sign
-    high = parity_sign((local >> 7) & lane)
-    for chunk in range(chunks):
-        matrix[:, chunk * LANES : (chunk + 1) * LANES] = (
-            low * high[:, chunk : chunk + 1]
-        ).astype(jnp.bfloat16)
-    out_ref[...] = jnp.dot(
-        matrix[...], scaled_ref[...], preferred_element_type=jnp.float32
+def front_kernel(
+    steps, picks_ref, picks_sign_ref, design_ref, weights_ref, labels_ref, signs_ref,
+    margins_ref, grad_ref, out_ref, matrix, mixed,
+):
+    step = pl.program_id(0)
+    block, width = design_ref.shape
+    tiles = width // LANES
+
+    @pl.when(step == 0)
+    def prepare():
+        row = lax.broadcasted_iota(jnp.int32, (block, block), 0)
+        col = lax.broadcasted_iota(jnp.int32, (block, block), 1)
+        matrix[...] = parity_sign(row & col).astype(jnp.bfloat16)
+        grad_ref[...] = jnp.zeros_like(grad_ref)
+
+    weights = jnp.broadcast_to(weights_ref[...], (LANES, width)).astype(jnp.bfloat16)
+    spread = lax.dot_general(
+        design_ref[...], weights, (((1,), (1,)), ((), ())), preferred_element_type=jnp.float32
     )
-
-
-def sampled_transform(picks, scaled):
-    rows_here, width = scaled.shape
+    parts = []
+    for piece in range(block // LANES):
+        span = slice(piece * LANES, (piece + 1) * LANES)
+        margin = spread[span, :].T[:8, :]
+        margins_ref[0, piece : piece + 1, :] = margin[:1, :]
+        prob = 1.0 / (1.0 + jnp.exp(-margin))
+        label = labels_ref[0, piece : piece + 1, :].astype(jnp.float32)
+        sign = signs_ref[0, piece : piece + 1, :].astype(jnp.float32)
+        misfit = (prob - label).astype(jnp.bfloat16)
+        grad_ref[...] += jnp.dot(
+            misfit, design_ref[span, :], preferred_element_type=jnp.float32
+        )
+        factor = ((1.0 - 2.0 * sign) * jnp.sqrt(prob * (1.0 - prob)))[:1, :]
+        column = jnp.broadcast_to(factor, (LANES, LANES)).T
+        wide = jnp.concatenate([column] * tiles, axis=1)
+        parts.append((design_ref[span, :].astype(jnp.float32) * wide).astype(jnp.bfloat16))
+    scaled = jnp.concatenate(parts, axis=0)
+    mixed[pl.ds(pl.multiple_of(step * block, block), block), :] = jnp.dot(
+        matrix[...], scaled, preferred_element_type=jnp.float32
+    )
+
+    @pl.when(step == steps - 1)
+    def finish():
+        @pl.loop(0, block // 8)
+        def butterfly(group):
+            for tile in range(tiles):
+                cols = slice(tile * LANES, (tile + 1) * LANES)
+                spots = [
+                    pl.ds(pl.multiple_of(index * block + group * 8, 8), 8)
+                    for index in range(steps)
+                ]
+                values = [mixed[spot, cols] for spot in spots]
+                gap = 1
+                while gap < steps:
+                    for index in range(steps):
+                        if not index & gap:
+                            above, below = values[index], values[index + gap]
+                            values[index] = above + below
+                            values[index + gap] = above - below
+                    gap *= 2
+                for spot, value in zip(spots, values):
+                    mixed[spot, cols] = value
+
+        @pl.loop(0, out_ref.shape[0] // 8)
+        def gather(group):
+            for lane in range(8):
+                place = group * 8 + lane
+                row = mixed[pl.ds(picks_ref[place], 1), :]
+                out_ref[pl.ds(place, 1), :] = row * picks_sign_ref[place]
+
+
+def front(design, weights, labels, signs, picks, picks_sign):
+    rows_here, width = design.shape
     total = picks.shape[0]
-    tile = 256
+    block = 256
+    steps = rows_here // block
+    lines = (steps, block // LANES, LANES)
+    smem = pl.BlockSpec(memory_space=pltpu.SMEM)
+    line = pl.BlockSpec((1,) + lines[1:], lambda i: (i, 0, 0))
     return pl.pallas_call(
-        functools.partial(sampled_kernel, rows_here),
-        grid=(total // tile,),
-        out_shape=jax.ShapeDtypeStruct((total, width), jnp.float32),
+        functools.partial(front_kernel, steps),
+        grid=(steps,),
+        out_shape=(
+            jax.ShapeDtypeStruct(lines, jnp.float32),
+            jax.ShapeDtypeStruct((8, width), jnp.float32),
+            jax.ShapeDtypeStruct((total, width), jnp.float32),
+        ),
         in_specs=[
-            pl.BlockSpec((tile, 1), lambda i: (i, 0)),
-            pl.BlockSpec((rows_here, width), lambda i: (0, 0)),
+            smem,
+            smem,
+            pl.BlockSpec((block, width), lambda i: (i, 0)),
+            pl.BlockSpec((1, width), lambda i: (0, 0)),
+            line,
+            line,
         ],
-        out_specs=pl.BlockSpec((tile, width), lambda i: (i, 0)),
-        scratch_shapes=[pltpu.VMEM((tile, rows_here), jnp.bfloat16)],
-        name="sampled_transform",
-    )(picks.reshape(total, 1), scaled)
+        out_specs=(
+            line,
+            pl.BlockSpec((8, width), lambda i: (0, 0)),
+            pl.BlockSpec((total, width), lambda i: (0, 0)),
+        ),
+        scratch_shapes=[
+            pltpu.VMEM((block, block), jnp.bfloat16),
+            pltpu.VMEM((rows_here, width), jnp.float32),
+        ],
+        name="front",
+    )(picks, picks_sign, design, weights.reshape(1, width), labels.reshape(lines), signs.reshape(lines))
 
 
 def allsum_kernel(count, own_ref, out_ref, slots, send_sem, recv_sem):
@@ -357,16 +427,14 @@
     rows_here, width = design.shape
     device_count = lax.axis_size("rows")
     total_rows = rows_here * device_count
-    margins = jnp.dot(design, weights.astype(jnp.bfloat16), preferred_element_type=jnp.float32)
-    prob = jax.nn.sigmoid(margins)
+    owner_sign = parity_sign((sample_rows // rows_here) & lax.axis_index("rows"))
+    margins, grad_part, own_part = front(
+        design, weights, labels, signs, sample_rows % rows_here, owner_sign
+    )
+    margins = margins.reshape(rows_here)
     target = labels.astype(jnp.float32)
-    misfit = (prob - target).astype(jnp.bfloat16)
-    grad_part = jnp.dot(misfit, design, preferred_element_type=jnp.float32)
-    factor_rows = (1.0 - 2.0 * signs.astype(jnp.float32)) * jnp.sqrt(prob * (1.0 - prob))
-    scaled = (design * factor_rows[:, None]).astype(jnp.bfloat16)
-    own_part = sampled_transform(sample_rows, scaled)
     piece, grad_sum = exchange(
-        own_part, grad_part.reshape(width // LANES, LANES), device_count
+        own_part, grad_part[0].reshape(width // LANES, LANES), device_count
     )
     gradient = grad_sum.reshape(width) / total_rows + ridge * weights
     newton_step = newton_solve(piece, gradient, total_rows)

time: 193 us -> 177 us (0.917)
  matrix products: 16.5 us -> 5.64 us
  other arithmetic: 12.6 us -> 5.15 us
  Pallas kernels: 161 us -> 163 us
    dot_general x2 -> x0, matrix products: 10.8 us -> none  [the longest x1 5.64 us: body(): jnp.dot(design, weights.astype(jnp.bfloat16), preferred_element_type=jnp....]
    convert_element_type x3 -> x1, other arithmetic: 8.75 us -> 1.32 us  [parity_sign(): return (1 - 2 * (bits & 1)).astype(jnp.float32)]
where the time goes in v3:
time: 177 us
  Pallas kernels  163 us (92%)
  matrix products  5.64 us (3%)
  other arithmetic  5.15 us (3%)
  local copies, waits for them, and re-layouts  2.06 us (1%)
    pallas_call x1, Pallas kernels, exchange(): pl.pallas_call(functools.partial(exchange_kernel, orders, spans), out_sha...  93.2 us
    pallas_call x1, Pallas kernels, front(): pl.pallas_call(functools.partial(front_kernel, steps), grid=(steps,), out...  34.4 us
    pallas_call x1, Pallas kernels, newton_solve(): pl.pallas_call(functools.partial(solve_kernel, total_rows), out_shape=jax...  25.3 us
    pallas_call x1, Pallas kernels, allsum(): pl.pallas_call(functools.partial(allsum_kernel, count), out_shape=jax.Sha...  10.2 us
    dot_general x1, matrix products, body(): jnp.dot(design, newton_step.astype(jnp.bfloat16), preferred_element_type=...  5.64 us

profile of v3, /device:TPU:0, one launch (start us, length us, event | category | flops | bytes accessed | tf_op | source)
XLA Modules:
  0.0 176.7 jit_solution(13618836485093339078)
XLA Ops:
  0.6 1.3 fusion.6
  2.0 0.0 copy-start.1
  2.0 34.4 %front.1 = (f32[16,2,128]{2,1,0:T(2,128)}, f32[8,1024]{1,0:T(8,128)}, f32[2048,1024]{1,0:T(8,128)}) custom-call(s32[2048]{0:T(1024)} %get-tuple-element.14.picks_ref, f32[2048]{0:T(1024)} %get-tuple-element.13.picks_sign_ref, bf16[4096,1024]{1,0:T(8,128)(2,1)} %design_ref.1, f32[1,1024]{1,0:T(1,128)} %bitcast.13, s32[16,2,128]{2,1,0:T(2,128)} %bitcast.12, ...), custom_call_target="tpu_custom_call" | custom-call | tf_op jit(solution)/shard_map/front/pallas_call | solution.py:100
  36.4 1.4 slice.6
  37.7 93.2 %exchange.1 = (bf16[2048,1024]{1,0:T(8,128)(2,1)}, f32[8,128]{1,0:T(8,128)}) custom-call(f32[2048,1024]{1,0:T(8,128)} %get-tuple-element.8.part_ref, f32[8,128]{1,0:T(8,128)} %bitcast.19), custom_call_target="tpu_custom_call" | custom-call | tf_op jit(solution)/shard_map/exchange/pallas_call | solution.py:326
  131.0 0.0 copy-start
  131.0 0.0 copy-start.3
  131.0 0.0 copy-start.4
  131.0 0.0 copy-done.1
  131.0 1.3 bitcast_add_fusion
  132.3 25.3 %newton_solve.1 = f32[1,1024]{1,0:T(1,128)} custom-call(bf16[2048,1024]{1,0:T(8,128)(2,1)} %get-tuple-element.11.piece_ref, f32[1,1024]{1,0:T(1,128)} %bitcast.20), custom_call_target="tpu_custom_call" | custom-call | tf_op jit(solution)/shard_map/newton_solve/pallas_call | solution.py:416
  157.6 0.0 copy-start.2
  157.6 0.8 convert_element_type.12
  158.3 5.6 %fusion.9 = f32[1,4096]{1,0:T(1,128)S(1)} fusion(bf16[1024,1]{0,1:T(2,128)(2,1)S(1)} %reshape.37, bf16[4096,1024]{1,0:T(8,128)(2,1)} %design_ref.1), kind=kOutput, calls=%fused_computation.26 | convolution fusion | flops 8388608 | bytes 8407040 | tf_op jit(solution)/shard_map/dot_general | solution.py:441
  164.0 0.0 copy-done
  164.0 0.0 copy-done.3
  164.0 0.0 copy-done.4
  164.0 0.3 subtract_reduce_fusion
  164.3 0.7 broadcast_in_dim.2.own_ref
  165.0 10.2 %allsum_1.1 = f32[8,128]{1,0:T(8,128)} custom-call(f32[8,128]{1,0:T(8,128)} %broadcast_in_dim.2.own_ref), custom_call_target="tpu_custom_call" | custom-call | tf_op jit(solution)/shard_map/allsum_1/pallas_call | solution.py:165
  175.2 0.8 multiply_reduce_fusion.1
  175.9 0.0 copy-done.2
  175.9 0.2 multiply_reduce_fusion
  176.1 0.5 multiply_add_fusion
  (3 shorter events, 0.0 us)
Async XLA Ops:
  2.0 129.0 %copy-start.1 = (f32[1024]{0:T(1024)S(1)}, f32[1024]{0:T(1024)}, u32[]{:S(2)}) copy-start(f32[1024]{0:T(1024)} %param.7) | copy-start | bytes 12292
  131.0 33.0 %copy-start = (s32[4096]{0:T(1024)S(1)}, s32[4096]{0:T(1024)}, u32[]{:S(2)}) copy-start(s32[4096]{0:T(1024)} %param.8) | copy-start | bytes 49156
  131.0 33.0 %copy-start.3 = (f32[4]{0:T(128)S(1)}, f32[4]{0:T(128)}, u32[]{:S(2)}) copy-start(f32[4]{0:T(128)} %constant.57.clone) | copy-start | bytes 52
  131.0 33.0 %copy-start.4 = (f32[16,2,128]{2,1,0:T(2,128)S(1)}, f32[16,2,128]{2,1,0:T(2,128)}, u32[]{:S(2)}) copy-start(f32[16,2,128]{2,1,0:T(2,128)} %get-tuple-element.12) | copy-start | bytes 49156
  157.6 18.4 %copy-start.2 = (f32[1,1024]{1,0:T(1,128)S(1)}, f32[1,1024]{1,0:T(1,128)}, u32[]{:S(2)}) copy-start(f32[1,1024]{1,0:T(1,128)} %newton_solve.1) | copy-start | bytes 12292

commit v4 on v3

--- a/solution.py
+++ b/solution.py
@@ -126,61 +126,100 @@
     )(picks, picks_sign, design, weights.reshape(1, width), labels.reshape(lines), signs.reshape(lines))
 
 
-def allsum_kernel(count, own_ref, out_ref, slots, send_sem, recv_sem):
+def tail_kernel(
+    steps, count, design_ref, newton_ref, margins_ref, labels_ref, out_ref,
+    held, slots, send_sem, recv_sem,
+):
+    step = pl.program_id(0)
     me = lax.axis_index("rows")
+    block, width = design_ref.shape
     barrier = pltpu.get_barrier_semaphore()
 
-    @pl.loop(1, count)
-    def greet(step):
-        pl.semaphore_signal(
-            barrier, inc=1, device_id=(lax.rem(me + step, count),), device_id_type=MESH
-        )
-
-    pl.semaphore_wait(barrier, count - 1)
-
-    def copy(step):
-        return pltpu.make_async_remote_copy(
-            src_ref=own_ref,
-            dst_ref=slots.at[me],
-            send_sem=send_sem.at[step],
-            recv_sem=recv_sem.at[step],
-            device_id=(lax.rem(me + step, count),),
-            device_id_type=MESH,
-        )
-
-    @pl.loop(1, count)
-    def send(step):
-        copy(step).start()
-
-    slots[me] = own_ref[...]
-
-    @pl.loop(1, count)
-    def finish(step):
-        copy(step).wait()
-
-    out_ref[...] = jnp.sum(slots[...], axis=0)
-
-
-def allsum(own, count, ident):
+    @pl.when(step == 0)
+    def enter():
+        held[...] = jnp.zeros_like(held)
+
+        @pl.loop(1, count)
+        def greet(turn):
+            pl.semaphore_signal(
+                barrier, inc=1, device_id=(lax.rem(me + turn, count),), device_id_type=MESH
+            )
+
+    newton = jnp.broadcast_to(newton_ref[...], (LANES, width)).astype(jnp.bfloat16)
+    spread = lax.dot_general(
+        design_ref[...], newton, (((1,), (1,)), ((), ())), preferred_element_type=jnp.float32
+    )
+    sub = lax.broadcasted_iota(jnp.int32, (8, LANES), 0)
+    length = jnp.where(sub == 0, 1.0, jnp.where(sub == 1, 0.5, jnp.where(sub == 2, 0.25, 0.125)))
+    loss = jnp.zeros((8, LANES), jnp.float32)
+    for piece in range(block // LANES):
+        along = spread[piece * LANES : (piece + 1) * LANES, :].T[:8, :]
+        trial = margins_ref[0, piece : piece + 1, :] - length * along
+        label = labels_ref[0, piece : piece + 1, :].astype(jnp.float32)
+        soft = jnp.maximum(trial, 0.0) + jnp.log1p(jnp.exp(-jnp.abs(trial)))
+        loss = loss + (soft - label * trial)
+    held[...] += loss
+
+    @pl.when(step == steps - 1)
+    def combine():
+        held[...] = jnp.broadcast_to(jnp.sum(held[...], axis=1, keepdims=True), (8, LANES))
+        pl.semaphore_wait(barrier, count - 1)
+
+        def copy(turn):
+            return pltpu.make_async_remote_copy(
+                src_ref=held,
+                dst_ref=slots.at[me],
+                send_sem=send_sem.at[turn],
+                recv_sem=recv_sem.at[turn],
+                device_id=(lax.rem(me + turn, count),),
+                device_id_type=MESH,
+            )
+
+        @pl.loop(1, count)
+        def send(turn):
+            copy(turn).start()
+
+        slots[me] = held[...]
+
+        @pl.loop(1, count)
+        def finish(turn):
+            copy(turn).wait()
+
+        out_ref[...] = jnp.sum(slots[...], axis=0)
+
+
+def tail(design, newton_step, margins, labels, count):
+    rows_here, width = design.shape
+    block = 512
+    steps = rows_here // block
+    lines = (steps, block // LANES, LANES)
+    line = pl.BlockSpec((1,) + lines[1:], lambda i: (i, 0, 0))
     return pl.pallas_call(
-        functools.partial(allsum_kernel, count),
-        out_shape=jax.ShapeDtypeStruct(own.shape, jnp.float32),
-        in_specs=[pl.BlockSpec(memory_space=pltpu.VMEM)],
-        out_specs=pl.BlockSpec(memory_space=pltpu.VMEM),
+        functools.partial(tail_kernel, steps, count),
+        grid=(steps,),
+        out_shape=jax.ShapeDtypeStruct((8, LANES), jnp.float32),
+        in_specs=[
+            pl.BlockSpec((block, width), lambda i: (i, 0)),
+            pl.BlockSpec((1, width), lambda i: (0, 0)),
+            line,
+            line,
+        ],
+        out_specs=pl.BlockSpec((8, LANES), lambda i: (0, 0)),
         scratch_shapes=[
-            pltpu.VMEM((count,) + own.shape, jnp.float32),
+            pltpu.VMEM((8, LANES), jnp.float32),
+            pltpu.VMEM((count, 8, LANES), jnp.float32),
             pltpu.SemaphoreType.DMA((count,)),
             pltpu.SemaphoreType.DMA((count,)),
         ],
-        compiler_params=pltpu.CompilerParams(collective_id=ident, has_side_effects=True),
-        name="allsum_%d" % ident,
-    )(own)
+        compiler_params=pltpu.CompilerParams(collective_id=1, has_side_effects=True),
+        name="tail",
+    )(design, newton_step.reshape(1, width), margins.reshape(lines), labels.reshape(lines))
 
 
 def exchange_kernel(
     orders, spans, part_ref, grad_ref, sketch_ref, gsum_ref,
     total, arrive_first, arrive_rest, grad_slots, grad_own,
-    send_sem, recv_sem, back_send, back_recv, grad_send, grad_recv,
+    send_sem, recv_sem, back_send, back_recv, grad_send, grad_recv, own_sem,
 ):
     me = lax.axis_index("rows")
     steps = len(orders[0])
@@ -195,6 +234,18 @@
     def mine(bit):
         return (me >> bit) & 1
 
+    core = orders[0][0]
+    base = pl.multiple_of(mine(core) * half, half)
+    other = pl.multiple_of((1 - mine(core)) * half, half)
+    own_copies = []
+    for group in groups:
+        cols = slice(*spans[group])
+        own_copies.append(
+            pltpu.make_async_copy(
+                part_ref.at[pl.ds(base, half), cols], total.at[:, cols], own_sem.at[group]
+            )
+        )
+        own_copies[group].start()
     barrier = pltpu.get_barrier_semaphore()
     for bit in range(steps):
         pl.semaphore_signal(barrier, inc=1, device_id=(peer(bit),), device_id_type=MESH)
@@ -206,9 +257,6 @@
             device_id=(peer(bit),), device_id_type=MESH,
         )
 
-    core = orders[0][0]
-    base = pl.multiple_of(mine(core) * half, half)
-    other = pl.multiple_of((1 - mine(core)) * half, half)
     sent = []
     pending = {}
 
@@ -266,7 +314,8 @@
             cols = slice(*spans[group])
             pending[(step, group)].wait_recv()
             if step == 0:
-                total[:, cols] = part_ref[pl.ds(base, half), cols] + arrive_first[:, cols]
+                own_copies[group].wait()
+                total[:, cols] = total[:, cols] + arrive_first[:, cols]
             else:
                 size = half >> step
                 place = half - (half >> (step - 1))
@@ -329,7 +378,7 @@
             jax.ShapeDtypeStruct((rows, width), jnp.bfloat16),
             jax.ShapeDtypeStruct(grad.shape, jnp.float32),
         ),
-        in_specs=[vmem, vmem],
+        in_specs=[pl.BlockSpec(memory_space=pl.ANY), vmem],
         out_specs=(vmem, vmem),
         scratch_shapes=[
             pltpu.VMEM((rows // 2, width), jnp.float32),
@@ -338,6 +387,7 @@
             pltpu.VMEM((bits,) + grad.shape, jnp.float32),
             pltpu.VMEM((bits,) + grad.shape, jnp.float32),
             grid_sem, grid_sem, grid_sem, grid_sem, line_sem, line_sem,
+            pltpu.SemaphoreType.DMA((lanes,)),
         ],
         compiler_params=pltpu.CompilerParams(collective_id=2, has_side_effects=True),
         name="exchange",
@@ -431,20 +481,13 @@
     margins, grad_part, own_part = front(
         design, weights, labels, signs, sample_rows % rows_here, owner_sign
     )
-    margins = margins.reshape(rows_here)
-    target = labels.astype(jnp.float32)
     piece, grad_sum = exchange(
         own_part, grad_part[0].reshape(width // LANES, LANES), device_count
     )
     gradient = grad_sum.reshape(width) / total_rows + ridge * weights
     newton_step = newton_solve(piece, gradient, total_rows)
-    along = jnp.dot(design, newton_step.astype(jnp.bfloat16), preferred_element_type=jnp.float32)
     lengths = jnp.array([1.0, 0.5, 0.25, 0.125], jnp.float32)
-    trial = margins[None, :] - lengths[:, None] * along[None, :]
-    row_loss = jnp.logaddexp(0.0, trial) - target[None, :] * trial
-    loss_part = jnp.sum(row_loss, axis=1)
-    loss_tile = jnp.broadcast_to(jnp.pad(loss_part, (0, 4))[:, None], (8, LANES))
-    loss_total = allsum(loss_tile, device_count, 1)[:4, 0]
+    loss_total = tail(design, newton_step, margins, labels, device_count)[:4, 0]
     moved = weights[None, :] - lengths[:, None] * newton_step[None, :]
     losses = loss_total / total_rows + 0.5 * ridge * jnp.sum(moved * moved, axis=1)
     return (gradient, newton_step, losses)

time: 177 us -> 170 us (0.960)
  matrix products: 5.64 us -> 0 us
    dot_general x1 -> x0, matrix products: 5.64 us -> none  [body(): jnp.dot(design, newton_step.astype(jnp.bfloat16), preferred_element_type=...]
    pallas_call x1, Pallas kernels: 10.2 us -> 14.2 us  [tail(): pl.pallas_call(functools.partial(tail_kernel, steps, count), grid=(steps,...]
    pallas_call x1, Pallas kernels: 93.2 us -> 90.7 us  [exchange(): pl.pallas_call(functools.partial(exchange_kernel, orders, spans), out_sha...]
where the time goes in v4:
time: 170 us; the launch traced here: 169 us
  Pallas kernels  163 us (96%)
  other arithmetic  4.09 us (2%)
    pallas_call x1, Pallas kernels, exchange(): pl.pallas_call(functools.partial(exchange_kernel, orders, spans), out_sha...  90.7 us
    pallas_call x1, Pallas kernels, front(): pl.pallas_call(functools.partial(front_kernel, steps), grid=(steps,), out...  34.4 us
    pallas_call x1, Pallas kernels, newton_solve(): pl.pallas_call(functools.partial(solve_kernel, total_rows), out_shape=jax...  23.6 us
    pallas_call x1, Pallas kernels, tail(): pl.pallas_call(functools.partial(tail_kernel, steps, count), grid=(steps,...  14.2 us

profile of v4, /device:TPU:0, one launch (start us, length us, event | category | flops | bytes accessed | tf_op | source)
XLA Modules:
  0.0 169.0 jit_solution(6058991717325547998)
XLA Ops:
  0.6 1.3 fusion.4
  2.0 0.0 copy-start.1
  2.0 34.4 %front.1 = (f32[16,2,128]{2,1,0:T(2,128)}, f32[8,1024]{1,0:T(8,128)}, f32[2048,1024]{1,0:T(8,128)}) custom-call(s32[2048]{0:T(1024)} %get-tuple-element.14.picks_ref, f32[2048]{0:T(1024)} %get-tuple-element.13.picks_sign_ref, bf16[4096,1024]{1,0:T(8,128)(2,1)} %design_ref.3, f32[1,1024]{1,0:T(1,128)} %bitcast.14, s32[16,2,128]{2,1,0:T(2,128)} %bitcast.10, ...), custom_call_target="tpu_custom_call" | custom-call | tf_op jit(solution)/shard_map/front/pallas_call | solution.py:100
  36.4 1.4 slice.6
  37.7 90.7 %exchange.1 = (bf16[2048,1024]{1,0:T(8,128)(2,1)}, f32[8,128]{1,0:T(8,128)}) custom-call(f32[2048,1024]{1,0:T(8,128)} %get-tuple-element.8.part_ref, f32[8,128]{1,0:T(8,128)} %bitcast.17), custom_call_target="tpu_custom_call" | custom-call | tf_op jit(solution)/shard_map/exchange/pallas_call | solution.py:375
  128.5 0.0 copy-start.2
  128.5 0.0 copy-done.1
  128.5 1.3 bitcast_add_fusion
  129.8 23.6 %newton_solve.1.newton_ref = f32[1,1024]{1,0:T(1,128)} custom-call(bf16[2048,1024]{1,0:T(8,128)(2,1)} %get-tuple-element.11.piece_ref, f32[1,1024]{1,0:T(1,128)} %bitcast.18), custom_call_target="tpu_custom_call" | custom-call | tf_op jit(solution)/shard_map/newton_solve/pallas_call | solution.py:466
  153.3 0.0 copy-start
  153.3 14.2 %tail.1 = f32[8,128]{1,0:T(8,128)} custom-call(bf16[4096,1024]{1,0:T(8,128)(2,1)} %design_ref.3, f32[1,1024]{1,0:T(1,128)} %newton_solve.1.newton_ref, f32[8,4,128]{2,1,0:T(4,128)} %bitcast.16, s32[8,4,128]{2,1,0:T(4,128)} %bitcast.11), custom_call_target="tpu_custom_call" | custom-call | tf_op jit(solution)/shard_map/tail/pallas_call | solution.py:197
  167.5 0.8 multiply_reduce_fusion.1
  168.3 0.0 copy-done.2
  168.3 0.0 copy-done
  168.3 0.2 multiply_reduce_fusion
  168.5 0.5 multiply_add_fusion
Async XLA Ops:
  2.0 126.5 %copy-start.1 = (f32[1024]{0:T(1024)S(1)}, f32[1024]{0:T(1024)}, u32[]{:S(2)}) copy-start(f32[1024]{0:T(1024)} %param.7) | copy-start | bytes 12292
  128.5 39.8 %copy-start.2 = (f32[4]{0:T(128)S(1)}, f32[4]{0:T(128)}, u32[]{:S(2)}) copy-start(f32[4]{0:T(128)} %constant.54.clone) | copy-start | bytes 52
  153.3 15.0 %copy-start = (f32[1,1024]{1,0:T(1,128)S(1)}, f32[1,1024]{1,0:T(1,128)}, u32[]{:S(2)}) copy-start(f32[1,1024]{1,0:T(1,128)} %newton_solve.1.newton_ref) | copy-start | bytes 12292

commit v5 on v4

--- a/solution.py
+++ b/solution.py
@@ -21,7 +21,7 @@
 
 def front_kernel(
     steps, picks_ref, picks_sign_ref, design_ref, weights_ref, labels_ref, signs_ref,
-    margins_ref, grad_ref, out_ref, matrix, mixed,
+    margins_ref, grad_out_ref, out_ref, matrix, mixed, grad_ref,
 ):
     step = pl.program_id(0)
     block, width = design_ref.shape
@@ -81,12 +81,24 @@
                 for spot, value in zip(spots, values):
                     mixed[spot, cols] = value
 
+        grad_out_ref[...] = grad_ref[:1, :]
+
         @pl.loop(0, out_ref.shape[0] // 8)
         def gather(group):
+            first = pl.multiple_of(group * 8, 8)
+            cut = width // 2
+            spots = [picks_ref[first + lane] for lane in range(8)]
+            sub = lax.broadcasted_iota(jnp.int32, (8, cut), 0)
+            sign = jnp.zeros((8, cut), jnp.float32)
             for lane in range(8):
-                place = group * 8 + lane
-                row = mixed[pl.ds(picks_ref[place], 1), :]
-                out_ref[pl.ds(place, 1), :] = row * picks_sign_ref[place]
+                sign = jnp.where(sub == lane, picks_sign_ref[first + lane], sign)
+            for start in (0, cut):
+                cols = slice(start, start + cut)
+                rows = jnp.zeros((8, cut), jnp.float32)
+                for lane in range(8):
+                    row = jnp.broadcast_to(mixed[pl.ds(spots[lane], 1), cols], (8, cut))
+                    rows = jnp.where(sub == lane, row, rows)
+                out_ref[pl.ds(first, 8), cols] = rows * sign
 
 
 def front(design, weights, labels, signs, picks, picks_sign):
@@ -102,7 +114,7 @@
         grid=(steps,),
         out_shape=(
             jax.ShapeDtypeStruct(lines, jnp.float32),
-            jax.ShapeDtypeStruct((8, width), jnp.float32),
+            jax.ShapeDtypeStruct((1, width), jnp.float32),
             jax.ShapeDtypeStruct((total, width), jnp.float32),
         ),
         in_specs=[
@@ -115,12 +127,13 @@
         ],
         out_specs=(
             line,
-            pl.BlockSpec((8, width), lambda i: (0, 0)),
+            pl.BlockSpec((1, width), lambda i: (0, 0)),
             pl.BlockSpec((total, width), lambda i: (0, 0)),
         ),
         scratch_shapes=[
             pltpu.VMEM((block, block), jnp.bfloat16),
             pltpu.VMEM((rows_here, width), jnp.float32),
+            pltpu.VMEM((8, width), jnp.float32),
         ],
         name="front",
     )(picks, picks_sign, design, weights.reshape(1, width), labels.reshape(lines), signs.reshape(lines))
@@ -362,12 +375,11 @@
     bits = count.bit_length() - 1
     rest = list(range(1, bits))
     tiles = width // LANES
-    lanes = 3
-    cuts = [-(-tiles * group // lanes) * LANES for group in range(lanes + 1)]
-    spans = [(cuts[group], cuts[group + 1]) for group in range(lanes)]
+    lanes = tiles
+    spans = [(group * LANES, (group + 1) * LANES) for group in range(lanes)]
     orders = []
     for group in range(lanes):
-        turn = group * len(rest) // lanes
+        turn = (group % 3) * len(rest) // 3
         orders.append([0] + rest[turn:] + rest[:turn])
     grid_sem = pltpu.SemaphoreType.DMA((bits, lanes))
     line_sem = pltpu.SemaphoreType.DMA((bits,))
@@ -394,7 +406,10 @@
     )(part, grad)
 
 
-def solve_kernel(total_rows, piece_ref, gradient_ref, step_ref, hess, vec_r, vec_p, vec_q):
+def solve_kernel(
+    total_rows, piece_ref, gsum_ref, weights_ref, gradient_ref, step_ref,
+    hess, vec_r, vec_p, vec_q,
+):
     width = piece_ref.shape[1]
     block = 256
     scale = 1.0 / total_rows
@@ -416,7 +431,8 @@
             jnp.where(row == col, hess[start : start + block, :], 0.0), axis=0, keepdims=True
         )
     inverse = 1.0 / diag
-    right = gradient_ref[...]
+    right = gsum_ref[...] * scale + ridge * weights_ref[...]
+    gradient_ref[...] = right
     vec_r[...] = right
     start_z = right * inverse
     vec_p[...] = start_z
@@ -460,17 +476,20 @@
     lax.while_loop(go, advance, (jnp.int32(0), jnp.max(start_rz), start_rz))
 
 
-def newton_solve(piece, gradient, total_rows):
+def newton_solve(piece, grad_sum, weights, total_rows):
     width = piece.shape[1]
     vector = pltpu.VMEM((1, width), jnp.float32)
-    return pl.pallas_call(
+    line = jax.ShapeDtypeStruct((1, width), jnp.float32)
+    vmem = pl.BlockSpec(memory_space=pltpu.VMEM)
+    gradient, step = pl.pallas_call(
         functools.partial(solve_kernel, total_rows),
-        out_shape=jax.ShapeDtypeStruct((1, width), jnp.float32),
-        in_specs=[pl.BlockSpec(memory_space=pltpu.VMEM)] * 2,
-        out_specs=pl.BlockSpec(memory_space=pltpu.VMEM),
+        out_shape=(line, line),
+        in_specs=[vmem] * 3,
+        out_specs=(vmem, vmem),
         scratch_shapes=[pltpu.VMEM((width, width), jnp.float32), vector, vector, vector],
         name="newton_solve",
-    )(piece, gradient.reshape(1, width)).reshape(width)
+    )(piece, grad_sum, weights.reshape(1, width))
+    return gradient.reshape(width), step.reshape(width)
 
 
 def body(design, weights, labels, signs, sample_rows):
@@ -481,11 +500,8 @@
     margins, grad_part, own_part = front(
         design, weights, labels, signs, sample_rows % rows_here, owner_sign
     )
-    piece, grad_sum = exchange(
-        own_part, grad_part[0].reshape(width // LANES, LANES), device_count
-    )
-    gradient = grad_sum.reshape(width) / total_rows + ridge * weights
-    newton_step = newton_solve(piece, gradient, total_rows)
+    piece, grad_sum = exchange(own_part, grad_part, device_count)
+    gradient, newton_step = newton_solve(piece, grad_sum, weights, total_rows)
     lengths = jnp.array([1.0, 0.5, 0.25, 0.125], jnp.float32)
     loss_total = tail(design, newton_step, margins, labels, device_count)[:4, 0]
     moved = weights[None, :] - lengths[:, None] * newton_step[None, :]

time: 170 us -> 153 us (0.900); the launches traced: 169 us -> 154 us
  Pallas kernels: 163 us -> 150 us
    pallas_call x1, Pallas kernels: 90.7 us -> 75.8 us  [exchange(): pl.pallas_call(functools.partial(exchange_kernel, orders, spans), out_sha...]
    pallas_call x1, Pallas kernels: 23.6 us -> 25.9 us  [newton_solve(): pl.pallas_call(functools.partial(solve_kernel, total_rows), out_shape=(li...]
where the time goes in v5:
time: 153 us; the launch traced here: 154 us
  Pallas kernels  150 us (98%)
  other arithmetic  2.82 us (2%)
    pallas_call x1, Pallas kernels, exchange(): pl.pallas_call(functools.partial(exchange_kernel, orders, spans), out_sha...  75.8 us
    pallas_call x1, Pallas kernels, front(): pl.pallas_call(functools.partial(front_kernel, steps), grid=(steps,), out...  33.4 us
    pallas_call x1, Pallas kernels, newton_solve(): pl.pallas_call(functools.partial(solve_kernel, total_rows), out_shape=(li...  25.9 us
    pallas_call x1, Pallas kernels, tail(): pl.pallas_call(functools.partial(tail_kernel, steps, count), grid=(steps,...  15.2 us

profile of v5, /device:TPU:0, one launch (start us, length us, event | category | flops | bytes accessed | tf_op | source)
XLA Modules:
  0.0 153.9 jit_solution(4248646279622072344)
XLA Ops:
  0.6 1.3 fusion.4
  2.0 33.4 %front.1 = (f32[16,2,128]{2,1,0:T(2,128)}, f32[1,1024]{1,0:T(1,128)}, f32[2048,1024]{1,0:T(8,128)}) custom-call(s32[2048]{0:T(1024)} %get-tuple-element.18.picks_ref, f32[2048]{0:T(1024)} %get-tuple-element.17.picks_sign_ref, bf16[4096,1024]{1,0:T(8,128)(2,1)} %design_ref.3, f32[1,1024]{1,0:T(1,128)} %bitcast.9, s32[16,2,128]{2,1,0:T(2,128)} %bitcast.7, ...), custom_call_target="tpu_custom_call" | custom-call | tf_op jit(solution)/shard_map/front/pallas_call | solution.py:112
  35.4 75.8 %exchange.1 = (bf16[2048,1024]{1,0:T(8,128)(2,1)}, f32[1,1024]{1,0:T(1,128)}) custom-call(f32[2048,1024]{1,0:T(8,128)} %get-tuple-element.10.part_ref, f32[1,1024]{1,0:T(1,128)} %get-tuple-element.11.grad_ref), custom_call_target="tpu_custom_call" | custom-call | tf_op jit(solution)/shard_map/exchange/pallas_call | solution.py:387
  111.3 0.0 copy-start
  111.3 0.0 copy-start.2
  111.3 25.9 %newton_solve.1 = (f32[1,1024]{1,0:T(1,128)}, f32[1,1024]{1,0:T(1,128)}) custom-call(bf16[2048,1024]{1,0:T(8,128)(2,1)} %get-tuple-element.12.piece_ref, f32[1,1024]{1,0:T(1,128)} %get-tuple-element.13.gsum_ref, f32[1,1024]{1,0:T(1,128)} %bitcast.10), custom_call_target="tpu_custom_call" | custom-call | tf_op jit(solution)/shard_map/newton_solve/pallas_call | solution.py:484
  137.1 0.0 copy-start.1
  137.1 15.2 %tail.1 = f32[8,128]{1,0:T(8,128)} custom-call(bf16[4096,1024]{1,0:T(8,128)(2,1)} %design_ref.3, f32[1,1024]{1,0:T(1,128)} %get-tuple-element.15.newton_ref, f32[8,4,128]{2,1,0:T(4,128)} %bitcast.14, s32[8,4,128]{2,1,0:T(4,128)} %bitcast.8), custom_call_target="tpu_custom_call" | custom-call | tf_op jit(solution)/shard_map/tail/pallas_call | solution.py:210
  152.3 0.8 multiply_reduce_fusion.1
  153.1 0.0 copy-done
  153.1 0.0 copy-done.2
  153.1 0.0 copy-done.1
  153.1 0.2 multiply_reduce_fusion
  153.3 0.5 multiply_add_fusion
Async XLA Ops:
  111.3 41.9 %copy-start = (f32[1024]{0:T(1024)S(1)}, f32[1024]{0:T(1024)}, u32[]{:S(2)}) copy-start(f32[1024]{0:T(1024)} %param.7) | copy-start | bytes 12292
  111.3 41.9 %copy-start.2 = (f32[4]{0:T(128)S(1)}, f32[4]{0:T(128)}, u32[]{:S(2)}) copy-start(f32[4]{0:T(128)} %constant.50.clone) | copy-start | bytes 52
  137.1 16.0 %copy-start.1 = (f32[1,1024]{1,0:T(1,128)S(1)}, f32[1,1024]{1,0:T(1,128)}, u32[]{:S(2)}) copy-start(f32[1,1024]{1,0:T(1,128)} %get-tuple-element.15.newton_ref) | copy-start | bytes 12292
